TPU v7x, 256 devices: a whole 4x4x8 slice. The times are simulated.
256 devices in a mesh: row: 8 (over x, y_lo), col: 16 (over z, core), pair: 2 (over y_hi).
Axes of the slice: x: 4, y: 4 (y_hi: 2, y_lo: 2; y = y_hi * 2 + y_lo), z: 8, core: 2. Of those that a mesh axis runs over, the one named last changes fastest.
Arguments:
- integrals: bfloat16 [8192, 32768], P('row', 'col'), may hold values from -0.03125 to 0.03125
- kept_tiles: int32 [512, 2048], P('row', 'col'), may hold values 0 or 1
- amplitudes: bfloat16 [32768, 1536], P(('col', 'row'), 'pair'), may hold values from -6 to 6
- driver: bfloat16 [8192, 1536], P(('row', 'col', 'pair')), may hold values from -6 to 6
- vir_energy: float32 [8192], P(('row', 'col', 'pair')), may hold values from 1 to 3
- occ_energy: float32 [1536], replicated, may hold values from -1.5 to -0.25
- occ_coupling: bfloat16 [1536, 1536], replicated, may hold values from -0.15625 to 0.15625
Outputs:
- increment: float32 [8192, 1536], P(('row', 'col', 'pair'))
All inputs are finite; a program needn't handle non-finite values. No bound on the sum of `kept_tiles` on one device may be relied on, other than what follows from the above.
Results may differ from a plain program's by a relative error of at most 0.0011.
Values may be sent and summed in bfloat16 or wider, within the bound.
A program may use at most 64 MiB of HBM per device.

v0:
```python
import jax
import jax.numpy as jnp
from jax import lax
from jax.sharding import Mesh
from jax.sharding import PartitionSpec as P

ROW = ("row_0", "row_1")
COL_ROW = ("col", "row_0", "row_1")
ROW_COL_PAIR = ("row_0", "row_1", "col", "pair")


def whole_of(value, axes, dim):
    if not axes:
        return value
    nearer = lax.all_gather(value, axes[-1], axis=dim, tiled=True)
    return whole_of(nearer, axes[:-1], dim)


def per_device(integrals, kept_tiles, amplitudes, driver, vir_energy, occ_energy, occ_coupling):
    bra_rows, ket_cols = integrals.shape
    tile_count = kept_tiles.shape[0]
    tile_size = bra_rows // tile_count
    col_mask = jnp.repeat(kept_tiles, tile_size, axis=1).astype(jnp.bfloat16)
    screened = (integrals.reshape(tile_count, tile_size, ket_cols) * col_mask[:, None, :]).reshape(
        bra_rows, ket_cols
    )
    ladder = jnp.dot(screened, whole_of(amplitudes, ROW, 0), preferred_element_type=jnp.float32)
    summed = lax.psum_scatter(ladder, "col", scatter_dimension=0, tiled=True)
    gathered = lax.all_to_all(summed, "pair", split_axis=0, concat_axis=1, tiled=True)
    residual = driver.astype(jnp.float32) + gathered
    denom = vir_energy[:, None] - occ_energy[None, :]
    scaled = (residual / denom).astype(jnp.bfloat16)
    coupled = jnp.dot(scaled, occ_coupling, preferred_element_type=jnp.float32)
    return -(residual - coupled) / denom


def solution(mesh):
    finer = Mesh(
        mesh.devices.reshape(4, 2, mesh.shape["col"], mesh.shape["pair"]),
        ("row_0", "row_1", "col", "pair"),
    )
    placed = (
        P(ROW, "col"),
        P(ROW, "col"),
        P(COL_ROW, "pair"),
        P(ROW_COL_PAIR, None),
        P(ROW_COL_PAIR),
        P(),
        P(),
    )
    return jax.shard_map(
        per_device, mesh=finer, in_specs=placed, out_specs=P(ROW_COL_PAIR, None), check_vma=False
    )
```

profile of v0, /device:TPU:2, one launch (start us, length us, event | category | flops | bytes accessed | tf_op | source)
XLA Modules:
  0.0 156.6 jit_solution(12972579513012139184)
XLA Ops:
  6.5 0.0 all-gather.2.cloned.1.call-start
  6.5 13.4 %all_gather.6 = bf16[512,768]{1,0:T(8,128)(2,1)} all-gather(bf16[256,768]{1,0:T(8,128)(2,1)} %param.9), channel_id=1, replica_groups=mesh['row_0'=4,'row_1'=2,'col'=16,'pair'=2] {'row_1'}, dimensions={0}, use_global_device_ids=true | all-gather | bytes 1179648 | tf_op jit(solution)/shard_map/all_gather | solution.py:15
  19.9 0.0 all-gather.2.cloned.1.call-update
  19.9 0.0 reduce-scatter.2.cloned.1.call-start
  20.0 0.8 convert_element_type.18
  20.7 0.1 copy.9
  20.9 0.1 broadcast_in_dim.2
  20.9 0.2 copy.10
  21.1 4.5 %bitcast_multiply_fusion = bf16[1024,2048]{1,0:T(8,128)(2,1)} fusion(bf16[1024,2048]{1,0:T(8,128)(2,1)} %param.7, bf16[64,2048]{1,0:T(8,128)(2,1)S(1)} %copy.10), kind=kLoop, calls=%fused_computation | loop fusion | flops 2097152 | bytes 8650752 | tf_op jit(solution)/shard_map/mul | solution.py:24
  25.6 0.0 copy-start
  25.6 0.0 copy-start.1
  25.6 0.0 copy-start.2
  25.6 38.4 %all-gather.2.cloned.1.call-done = bf16[2048,768]{1,0:T(8,128)(2,1)} async-done(((bf16[512,768]{1,0:T(8,128)(2,1)}), bf16[2048,768]{1,0:T(8,128)(2,1)}) %all-gather.2.cloned.1.call-update) | async-done | bytes 3145744 | tf_op jit(solution)/shard_map/all_gather | solution.py:15
  64.0 8.3 %fusion.8 = f32[1024,768]{1,0:T(8,128)} fusion(bf16[1024,2048]{1,0:T(8,128)(2,1)} %bitcast_multiply_fusion, bf16[2048,768]{1,0:T(8,128)(2,1)} %all-gather.2.cloned.1.call-done), kind=kOutput, calls=%fused_computation.10 | convolution fusion | flops 3221225472 | bytes 10485760 | tf_op jit(solution)/shard_map/dot_general | solution.py:27
  72.3 0.0 reduce-scatter.2.cloned.1.call-update
  72.3 62.8 %reduce-scatter.2.cloned.1.call-done = f32[64,768]{1,0:T(8,128)} async-done(((f32[1024,768]{1,0:T(8,128)}), f32[64,768]{1,0:T(8,128)}) %reduce-scatter.2.cloned.1.call-update) | async-done | bytes 196624 | tf_op jit(solution)/shard_map/reduce_scatter | solution.py:28
  135.1 10.6 %all_to_all.19 = f32[2,32,768]{2,1,0:T(8,128)S(1)} all-to-all(f32[2,32,768]{2,1,0:T(8,128)} %bitcast.13), channel_id=1, replica_groups=mesh['row_0'=4,'row_1'=2,'col'=16,'pair'=2] {'pair'}, dimensions={0} | all-to-all | bytes 393216 | tf_op jit(solution)/shard_map/all_to_all | solution.py:29
  145.7 0.0 copy-done
  145.7 0.0 copy-done.1
  145.7 0.0 copy-done.2
  145.7 4.0 %fusion.1 = f32[32,1536]{1,0:T(8,128)} fusion(bf16[1536,1536]{1,0:T(8,128)(2,1)} %param.13, f32[32,1536]{1,0:T(8,128)S(1)} %bitcast.11, bf16[32,1536]{1,0:T(8,128)(2,1)S(1)} %copy-done, f32[1536]{0:T(1024)S(1)} %copy-done.1, f32[32]{0:T(128)S(1)} %copy-done.2), kind=kOutput, calls=%fused_computation.3 | convolution fusion | flops 151535616 | bytes 5216384 | tf_op jit(solution)/shard_map/dot_general | solution.py:33
  (1 shorter events, 0.0 us)
Async XLA Ops:
  6.5 57.5 %all-gather.2.cloned.1.call-start = ((), (), s32[]{:S(2)}) async-start(), calls=%async_computation.2 | async-start | bytes 3932160 | tf_op jit(solution)/shard_map/all_gather | solution.py:15
  19.9 115.2 %reduce-scatter.2.cloned.1.call-start = ((), (), s32[]{:S(2)}) async-start(), calls=%async_computation.3 | async-start | bytes 3342336 | tf_op jit(solution)/shard_map/reduce_scatter | solution.py:28
  25.6 120.1 %copy-start = (bf16[32,1536]{1,0:T(8,128)(2,1)S(1)}, bf16[32,1536]{1,0:T(8,128)(2,1)}, u32[]{:S(2)}) copy-start(bf16[32,1536]{1,0:T(8,128)(2,1)} %param.10) | copy-start | bytes 294916
  25.6 120.1 %copy-start.1 = (f32[1536]{0:T(1024)S(1)}, f32[1536]{0:T(1024)}, u32[]{:S(2)}) copy-start(f32[1536]{0:T(1024)} %param.12) | copy-start | bytes 18436
  25.6 120.1 %copy-start.2 = (f32[32]{0:T(128)S(1)}, f32[32]{0:T(128)}, u32[]{:S(2)}) copy-start(f32[32]{0:T(128)} %param.11) | copy-start | bytes 388
Sparse Core Ops, SparseCore 0:
  20.0 43.9 all-gather.1
  72.4 62.5 reduce-scatter.1
where the time goes:
time: 157 us
  waiting for transfers between devices  101 us (64%)
  blocking collectives  24 us (15%)
  between operations  13.4 us (9%)
  matrix products  12.3 us (8%)
  other arithmetic  5.24 us (3%)
    reduce_scatter x1, waiting for transfers between devices, per_device(): summed = lax.psum_scatter(ladder, 'col', scatter_dimension=0, tiled=True)  62.8 us
    all_gather x1, waiting for transfers between devices, whole_of(): nearer = lax.all_gather(value, axes[-1], axis=dim, tiled=True)  38.4 us
    all_gather x1, blocking collectives, whole_of(): nearer = lax.all_gather(value, axes[-1], axis=dim, tiled=True)  13.4 us
    all_to_all x1, blocking collectives, per_device(): lax.all_to_all(summed, 'pair', split_axis=0, concat_axis=1, tiled=True)  10.6 us
    dot_general x1, matrix products, per_device(): jnp.dot(screened, whole_of(amplitudes, ROW, 0), preferred_element_type=jn...  8.28 us
    mul x1, other arithmetic, per_device(): integrals.reshape(tile_count, tile_size, ket_cols) * col_mask[:, None, :]  4.48 us
    dot_general x1, matrix products, per_device(): coupled = jnp.dot(scaled, occ_coupling, preferred_element_type=jnp.float32)  4 us
  transfers between devices with their start and end apart: 2, of which 2 were waited for; matrix products, arithmetic and copies ran while one was open for 4% of the time, Pallas kernels for 0%

commit v1 on v0

v1 whole, which is shorter than its diff:
```python
import jax
import jax.numpy as jnp
from jax import lax
from jax.experimental import pallas as pl
from jax.experimental.pallas import tpu as pltpu
from jax.sharding import PartitionSpec as P

MESH = pl.DeviceIdType.MESH
WIDTH = 128
FIRST = 112
HALF = 128
QUARTER = 64
AHEAD = 2
LEVELS = 32000.0


def kernel(
    integrals, kept, amplitudes, driver, vir, occ, coupling, out,
    screened, kept_v, driver_v, vir_v, occ_v, coup_v, mask, amps, part, sib, quant, scale, zin, zscale,
    total, pair_in, resid, coupled,
    load_sem, amp_sem, a_send, a_recv, d_send, d_recv, z_send, z_recv, s_send, s_recv, p_send, p_recv,
):
    chunks, rows, kets, width = amps.shape
    depth = screened.shape[1]
    sites = part.shape[1]
    row, col, pair = lax.axis_index("row"), lax.axis_index("col"), lax.axis_index("pair")
    x, y = row // 2, row % 2
    z, core = col // 2, col % 2
    ring = rows // 2

    def at(x_, y_):
        return lax.rem(x_ + ring, ring) * 2 + y_

    up, down, over = at(x + 1, y), at(x - 1, y), at(x, 1 - y)
    two = at(x + 2, y)
    up_o, down_o, two_o = at(x + 1, 1 - y), at(x - 1, 1 - y), at(x + 2, 1 - y)

    def peer(row_=None, col_=None, pair_=None):
        return (
            row if row_ is None else row_,
            col if col_ is None else col_,
            pair if pair_ is None else pair_,
        )

    to_up, to_down, to_over = peer(up), peer(down), peer(over)
    to_sib = peer(None, z * 2 + 1 - core)
    to_pair = peer(None, None, 1 - pair)

    def to_site(d):
        return peer(None, lax.rem(z + d, sites) * 2 + core)

    own_loads = []
    for j in range(chunks):
        c = pltpu.make_async_copy(
            amplitudes.at[:, pl.ds(j * width, width)], amps.at[j, row], amp_sem.at[j]
        )
        c.start()
        own_loads.append(c)
    pairs_ = (
        (kept, kept_v), (integrals, screened), (vir, vir_v), (occ, occ_v), (driver, driver_v), (coupling, coup_v),
    )
    loads = [pltpu.make_async_copy(a, b, load_sem.at[i]) for i, (a, b) in enumerate(pairs_)]
    for c in loads:
        c.start()

    barrier = pltpu.get_barrier_semaphore()
    friends = [to_up, to_down, to_over, to_sib, to_pair] + [to_site(d) for d in range(1, sites)]
    for f in friends:
        pl.semaphore_signal(barrier, inc=1, device_id=f, device_id_type=MESH)

    def hop(j, i, block, lo, hi, device):
        ref = amps.at[j, block, pl.ds(lo, hi - lo)]
        return pltpu.make_async_remote_copy(
            src_ref=ref, dst_ref=ref, send_sem=a_send.at[j, i], recv_sem=a_recv.at[j, i],
            device_id=device, device_id_type=MESH,
        )

    hops = (
        (row, down, 0, kets, to_up),
        (row, up, 0, kets, to_down),
        (row, over, 0, kets, to_over),
        (down, two, 0, HALF, to_up),
        (down, down_o, 0, FIRST, to_over),
        (up, two, HALF, kets, to_down),
        (up, up_o, 0, FIRST, to_over),
        (over, down_o, FIRST, kets, to_up),
        (over, up_o, FIRST, kets, to_down),
        (two, two_o, 0, FIRST, to_over),
        (down_o, two_o, FIRST, FIRST + QUARTER, to_up),
        (up_o, two_o, FIRST + QUARTER, kets, to_down),
    )

    def send(j, i):
        block, _, lo, hi, device = hops[i]
        hop(j, i, block, lo, hi, device).start()

    def arrived(j, i):
        _, block, lo, hi, device = hops[i]
        hop(j, i, block, lo, hi, device).wait_recv()

    def sent(j):
        for i, (block, _, lo, hi, device) in enumerate(hops):
            hop(j, i, block, lo, hi, device).wait_send()

    def first(j):
        own_loads[j].wait()
        for i in (0, 1, 2):
            send(j, i)

    def second(j):
        arrived(j, 0)
        send(j, 3)
        send(j, 4)
        arrived(j, 1)
        send(j, 5)
        send(j, 6)
        arrived(j, 2)
        send(j, 7)
        send(j, 8)

    def third(j):
        arrived(j, 7)
        send(j, 10)
        arrived(j, 8)
        send(j, 11)
        arrived(j, 3)
        send(j, 9)

    def gathered(j):
        for i in (4, 5, 6, 9, 10, 11):
            arrived(j, i)

    def sib_copy(j):
        return pltpu.make_async_remote_copy(
            src_ref=part.at[j, :, 1 - core], dst_ref=sib.at[j], send_sem=d_send.at[j], recv_sem=d_recv.at[j],
            device_id=to_sib, device_id_type=MESH,
        )

    def multiply(j):
        def step(m, carry):
            left = screened[pl.ds(m * 256, 256), :]
            right = amps[j].reshape(rows * kets, width)
            product = jnp.dot(left, right, preferred_element_type=jnp.float32)
            part[j, pl.ds(m * 2, 2)] = product.reshape(2, 2, 64, width)
            return carry

        lax.fori_loop(0, screened.shape[0] // 256, step, 0)
        sib_copy(j).start()

    def site_copy(j, d):
        return pltpu.make_async_remote_copy(
            src_ref=quant.at[j, d - 1], dst_ref=zin.at[j, d - 1],
            send_sem=z_send.at[j, d - 1], recv_sem=z_recv.at[j, d - 1],
            device_id=to_site(d), device_id_type=MESH,
        )

    def scale_copy(j, d):
        return pltpu.make_async_remote_copy(
            src_ref=scale.at[j, d - 1], dst_ref=zscale.at[j, d - 1],
            send_sem=s_send.at[j, d - 1], recv_sem=s_recv.at[j, d - 1],
            device_id=to_site(d), device_id_type=MESH,
        )

    order = sorted(range(1, sites), key=lambda d: -min(d, sites - d))

    def scatter(j):
        sib_copy(j).wait_recv()
        for d in order:
            dest = lax.rem(z + d, sites)
            value = part[j, dest, core] + sib[j, dest]
            top = jnp.maximum(jnp.max(jnp.abs(value), axis=0, keepdims=True), 1e-30)
            scale[j, d - 1] = top * (1.0 / LEVELS)
            quant[j, d - 1] = jnp.round(value * (LEVELS / top)).astype(jnp.int32).astype(jnp.int16)
            scale_copy(j, d).start()
            site_copy(j, d).start()

    def pair_copy(j):
        return pltpu.make_async_remote_copy(
            src_ref=total.at[j, pl.ds((1 - pair) * 32, 32)], dst_ref=pair_in.at[j],
            send_sem=p_send.at[j], recv_sem=p_recv.at[j],
            device_id=to_pair, device_id_type=MESH,
        )

    def collect(j):
        value = part[j, z, core] + sib[j, z]
        for d in reversed(order):
            scale_copy(j, d).wait_recv()
            site_copy(j, d).wait_recv()
            value += zin[j, d - 1].astype(jnp.int32).astype(jnp.float32) * zscale[j, d - 1]
        total[j] = value
        pair_copy(j).start()

    half = chunks * width

    def couple(j, which, ladder):
        columns = pl.ds(pl.multiple_of(which * half + j * width, width), width)
        residual = driver_v[:, columns].astype(jnp.float32) + ladder
        resid[:, columns] = residual
        scaled = (residual / (vir_col() - occ_v[:, columns])).astype(jnp.bfloat16)
        coupled[...] += jnp.dot(scaled, coup_v[columns, :], preferred_element_type=jnp.float32)

    def vir_col():
        n = vir_v.shape[1]
        eye = lax.broadcasted_iota(jnp.int32, (n, n), 0) == lax.broadcasted_iota(jnp.int32, (n, n), 1)
        return jnp.sum(jnp.where(eye, jnp.broadcast_to(vir_v[...], (n, n)), 0.0), axis=1, keepdims=True)

    def finish(j):
        couple(j, pair, total[j, pl.ds(pair * 32, 32)])
        pair_copy(j).wait_recv()
        couple(j, 1 - pair, pair_in[j])

    pl.semaphore_wait(barrier, len(friends))
    for j in range(min(AHEAD, chunks)):
        first(j)

    coupled[...] = jnp.zeros_like(coupled)
    loads[0].wait()
    tiles = kept_v.shape[1]
    tile = depth // tiles
    keep = kept_v[...].astype(jnp.float32).astype(jnp.bfloat16)
    for b in range(depth // 256):
        ket = lax.broadcasted_iota(jnp.int32, (tiles, 256), 1) + b * 256
        of = lax.broadcasted_iota(jnp.int32, (tiles, 256), 0) * tile
        spread = jnp.where((ket >= of) & (ket < of + tile), 1.0, 0.0).astype(jnp.bfloat16)
        mask[:, pl.ds(b * 256, 256)] = jnp.dot(keep, spread, preferred_element_type=jnp.float32)
    loads[1].wait()

    def screen(i, carry):
        strip = pl.ds(i * tile, tile)
        keep_row = jnp.broadcast_to(mask[pl.ds(i, 1), :], (tile, depth)).astype(jnp.bfloat16)
        screened[strip, :] = screened[strip, :] * keep_row
        return carry

    lax.fori_loop(0, kept_v.shape[0], screen, 0)

    for s in range(chunks + 2):
        if s < chunks:
            second(s)
        if 0 <= s - 1 < chunks:
            third(s - 1)
        if s + AHEAD < chunks:
            first(s + AHEAD)
        if s == 2:
            for c in loads[2:]:
                c.wait()
        if s >= 5:
            finish(s - 5)
        if s >= 4:
            collect(s - 4)
        if s >= 3:
            scatter(s - 3)
        if s >= 2:
            gathered(s - 2)
            multiply(s - 2)
            sent(s - 2)
    last = chunks - 1
    scatter(last)
    if chunks > 2:
        finish(last - 2)
    if chunks > 1:
        collect(last - 1)
        finish(last - 1)
    for j in range(chunks):
        sib_copy(j).wait_send()
        if j < last:
            pair_copy(j).wait_send()
        for d in order:
            site_copy(j, d).wait_send()
            scale_copy(j, d).wait_send()
    collect(last)
    finish(last)
    out[...] = resid[...] - coupled[...]
    pair_copy(last).wait_send()


def per_device(integrals, kept_tiles, amplitudes, driver, vir_energy, occ_energy, occ_coupling):
    bra, depth = integrals.shape
    kets, half = amplitudes.shape
    rows = depth // kets
    chunks = half // WIDTH
    sites = bra // 128
    own, whole = driver.shape
    any_ = pl.BlockSpec(memory_space=pl.ANY)
    dma = pltpu.SemaphoreType.DMA
    numerator = pl.pallas_call(
        kernel,
        out_shape=jax.ShapeDtypeStruct((own, whole), jnp.float32),
        in_specs=[any_] * 7,
        out_specs=pl.BlockSpec(memory_space=pltpu.VMEM),
        scratch_shapes=[
            pltpu.VMEM((bra, depth), jnp.bfloat16),
            pltpu.VMEM(kept_tiles.shape, jnp.int32),
            pltpu.VMEM((own, whole), jnp.bfloat16),
            pltpu.VMEM((1, own), jnp.float32),
            pltpu.VMEM((1, whole), jnp.float32),
            pltpu.VMEM((whole, whole), jnp.bfloat16),
            pltpu.VMEM((kept_tiles.shape[0], depth), jnp.float32),
            pltpu.VMEM((chunks, rows, kets, WIDTH), jnp.bfloat16),
            pltpu.VMEM((chunks, sites, 2, 64, WIDTH), jnp.float32),
            pltpu.VMEM((chunks, sites, 64, WIDTH), jnp.float32),
            pltpu.VMEM((chunks, sites - 1, 64, WIDTH), jnp.int16),
            pltpu.VMEM((chunks, sites - 1, 1, WIDTH), jnp.float32),
            pltpu.VMEM((chunks, sites - 1, 64, WIDTH), jnp.int16),
            pltpu.VMEM((chunks, sites - 1, 1, WIDTH), jnp.float32),
            pltpu.VMEM((chunks, 64, WIDTH), jnp.float32),
            pltpu.VMEM((chunks, 32, WIDTH), jnp.float32),
            pltpu.VMEM((own, whole), jnp.float32),
            pltpu.VMEM((own, whole), jnp.float32),
            dma((6,)),
            dma((chunks,)),
            dma((chunks, 12)),
            dma((chunks, 12)),
            dma((chunks,)),
            dma((chunks,)),
            dma((chunks, sites - 1)),
            dma((chunks, sites - 1)),
            dma((chunks, sites - 1)),
            dma((chunks, sites - 1)),
            dma((chunks,)),
            dma((chunks,)),
        ],
        compiler_params=pltpu.CompilerParams(
            collective_id=0, has_side_effects=True, vmem_limit_bytes=48 * 1024 * 1024
        ),
        name="ladder",
    )(
        integrals, kept_tiles, amplitudes, driver,
        vir_energy.reshape(1, own), occ_energy.reshape(1, whole), occ_coupling,
    )
    return -numerator / (vir_energy[:, None] - occ_energy[None, :])


def solution(mesh):
    place = ("row", "col", "pair")
    placed = (
        P("row", "col"),
        P("row", "col"),
        P(("col", "row"), "pair"),
        P(place, None),
        P(place),
        P(),
        P(),
    )
    return jax.shard_map(
        per_device, mesh=mesh, in_specs=placed, out_specs=P(place, None), check_vma=False
    )
```

time: 157 us -> 68.3 us (0.44)
  the two profiles are of different devices: /device:TPU:2 before, /device:TPU:1 now
where the time goes in v1:
time: 68.3 us; the launch traced here: 68 us
  Pallas kernels  61 us (89%)
  local copies, waits for them, and re-layouts  6.19 us (9%)
  other arithmetic  0.78 us (1%)
    pallas_call x1, Pallas kernels, per_device(): pl.pallas_call(kernel, out_shape=jax.ShapeDtypeStruct((own, whole), jnp.f...  61 us
    unnamed x12, local copies, waits for them, and re-layouts  5.49 us

profile of v1, /device:TPU:1, one launch (start us, length us, event | category | flops | bytes accessed | tf_op | source)
XLA Modules:
  0.0 68.0 jit_solution(14895291283606872669)
XLA Ops:
  0.0 0.7 %reshape.9.occ = f32[1,1536]{1,0:T(1,128)S(1)} reshape(f32[1536]{0:T(1024)} %param.12) | data formatting | bytes 12288 | tf_op jit(solution)/shard_map/reshape | solution.py:328
  0.7 0.0 copy-start
  0.7 2.2 %copy-done = bf16[1024,2048]{1,0:T(8,128)(2,1)S(1)} copy-done((bf16[1024,2048]{1,0:T(8,128)(2,1)S(1)}, bf16[1024,2048]{1,0:T(8,128)(2,1)}, u32[]{:S(2)}) %copy-start) | copy-done | bytes 4194328
  2.9 0.0 copy-start.1
  2.9 1.0 %copy-done.1 = bf16[256,768]{1,0:T(8,128)(2,1)S(1)} copy-done((bf16[256,768]{1,0:T(8,128)(2,1)S(1)}, bf16[256,768]{1,0:T(8,128)(2,1)}, u32[]{:S(2)}) %copy-start.1) | copy-done | bytes 393240
  3.9 0.0 copy-start.2
  3.9 0.9 %copy-done.2 = bf16[32,1536]{1,0:T(8,128)(2,1)S(1)} copy-done((bf16[32,1536]{1,0:T(8,128)(2,1)S(1)}, bf16[32,1536]{1,0:T(8,128)(2,1)}, u32[]{:S(2)}) %copy-start.2) | copy-done | bytes 98328
  4.8 0.0 copy-start.3
  4.8 0.8 %copy-done.3 = s32[64,128]{1,0:T(8,128)S(1)} copy-done((s32[64,128]{1,0:T(8,128)S(1)}, s32[64,128]{1,0:T(8,128)}, u32[]{:S(2)}) %copy-start.3) | copy-done | bytes 32792
  5.5 0.0 copy-start.4
  5.5 0.7 copy-done.4
  6.2 0.0 copy-start.5
  6.2 61.0 %ladder.1 = f32[32,1536]{1,0:T(8,128)S(1)} custom-call(bf16[1024,2048]{1,0:T(8,128)(2,1)S(1)} %copy-done, s32[64,128]{1,0:T(8,128)S(1)} %copy-done.3, bf16[256,768]{1,0:T(8,128)(2,1)S(1)} %copy-done.1, bf16[32,1536]{1,0:T(8,128)(2,1)S(1)} %copy-done.2, f32[1,32]{1,0:T(1,128)S(1)} %bitcast.1, f32[1,1536]{1,0:T(1,128)S(1)} %reshape.9.occ, ...), custom_call_target="tpu_custom_call" | custom-call | tf_op jit(solution)/shard_map/ladder/pallas_call | solution.py:285
  67.2 0.0 copy-done.5
  67.2 0.8 %subtract_divide_fusion = f32[32,1536]{1,0:T(8,128)} fusion(f32[32,1536]{1,0:T(8,128)S(1)} %ladder.1, f32[1536]{0:T(1024)S(1)} %copy-done.5, f32[32]{0:T(128)S(1)} %copy-done.4), kind=kLoop, calls=%fused_computation | loop fusion | flops 147456 | bytes 399488 | tf_op jit(solution)/shard_map/div | solution.py:330
Async XLA Ops:
  0.7 2.2 %copy-start = (bf16[1024,2048]{1,0:T(8,128)(2,1)S(1)}, bf16[1024,2048]{1,0:T(8,128)(2,1)}, u32[]{:S(2)}) copy-start(bf16[1024,2048]{1,0:T(8,128)(2,1)} %integrals.1) | copy-start | bytes 12582916
  2.9 1.0 %copy-start.1 = (bf16[256,768]{1,0:T(8,128)(2,1)S(1)}, bf16[256,768]{1,0:T(8,128)(2,1)}, u32[]{:S(2)}) copy-start(bf16[256,768]{1,0:T(8,128)(2,1)} %amplitudes.1) | copy-start | bytes 1179652
  3.9 0.9 %copy-start.2 = (bf16[32,1536]{1,0:T(8,128)(2,1)S(1)}, bf16[32,1536]{1,0:T(8,128)(2,1)}, u32[]{:S(2)}) copy-start(bf16[32,1536]{1,0:T(8,128)(2,1)} %driver.1) | copy-start | bytes 294916
  4.8 0.8 %copy-start.3 = (s32[64,128]{1,0:T(8,128)S(1)}, s32[64,128]{1,0:T(8,128)}, u32[]{:S(2)}) copy-start(s32[64,128]{1,0:T(8,128)} %kept.1) | copy-start | bytes 98308
  5.5 0.7 copy-start.4
  6.2 61.0 %copy-start.5 = (f32[1536]{0:T(1024)S(1)}, f32[1536]{0:T(1024)}, u32[]{:S(2)}) copy-start(f32[1536]{0:T(1024)} %param.12) | copy-start | bytes 18436

commit v2 on v1

v2 whole, which is shorter than its diff:
```python
import jax
import jax.numpy as jnp
from jax import lax
from jax.experimental import pallas as pl
from jax.experimental.pallas import tpu as pltpu
from jax.sharding import PartitionSpec as P

MESH = pl.DeviceIdType.MESH
WIDTH = 128
FIRST = 112
HALF = 128
QUARTER = 64
ORDER = "SFECXTG"
LAG_T = 1
LAG_G = 2
AHEAD = 2
LEVELS = 32000.0
GROUP = (0, 0, 0, 1, 2, 3, 2, 1, 1, 2, 3, 2)


def kernel(
    integrals, kept, amplitudes, driver, vir, occ, coupling, out,
    screened, kept_v, driver_v, vir_v, occ_v, coup_v, mask, amps, part, sib, quant, scale, zin, zscale,
    total, pair_in, resid, coupled,
    load_sem, sends, a_recv, d_recv, z_recv, s_recv, p_recv, ready,
):
    chunks, rows, kets, width = amps.shape
    depth = screened.shape[1]
    sites = part.shape[1]
    row, col, pair = lax.axis_index("row"), lax.axis_index("col"), lax.axis_index("pair")
    x, y = row // 2, row % 2
    z, core = col // 2, col % 2
    ring = rows // 2

    def at(x_, y_):
        return lax.rem(x_ + ring, ring) * 2 + y_

    up, down, over = at(x + 1, y), at(x - 1, y), at(x, 1 - y)
    two = at(x + 2, y)
    up_o, down_o, two_o = at(x + 1, 1 - y), at(x - 1, 1 - y), at(x + 2, 1 - y)

    def peer(row_=None, col_=None, pair_=None):
        return (
            row if row_ is None else row_,
            col if col_ is None else col_,
            pair if pair_ is None else pair_,
        )

    to_up, to_down, to_over = peer(up), peer(down), peer(over)
    to_sib = peer(None, z * 2 + 1 - core)
    to_pair = peer(None, None, 1 - pair)

    def to_site(d):
        return peer(None, lax.rem(z + d, sites) * 2 + core)

    for j in range(chunks):
        pltpu.make_async_copy(
            amplitudes.at[:, pl.ds(j * width, width)], amps.at[j, row], load_sem.at[6]
        ).start()
    pairs_ = (
        (kept, kept_v), (integrals, screened), (vir, vir_v), (occ, occ_v), (driver, driver_v), (coupling, coup_v),
    )
    loads = [pltpu.make_async_copy(a, b, load_sem.at[i]) for i, (a, b) in enumerate(pairs_)]
    for c in loads:
        c.start()

    barrier = pltpu.get_barrier_semaphore()
    friends = [to_up, to_down, to_over, to_sib, to_pair, to_site(1), to_site(sites - 1)]
    for f in friends:
        pl.semaphore_signal(barrier, inc=1, device_id=f, device_id_type=MESH)

    def tell(n):
        for d in (1, sites - 1):
            pl.semaphore_signal(ready.at[n], inc=1, device_id=to_site(d), device_id_type=MESH)

    def told(n):
        pl.semaphore_wait(ready.at[n], 2)

    def hop(j, i, block, lo, hi, device):
        ref = amps.at[j, block, pl.ds(lo, hi - lo)]
        return pltpu.make_async_remote_copy(
            src_ref=ref, dst_ref=ref, send_sem=sends.at[0], recv_sem=a_recv.at[j, GROUP[i]],
            device_id=device, device_id_type=MESH,
        )

    hops = (
        (row, down, 0, kets, to_up),
        (row, up, 0, kets, to_down),
        (row, over, 0, kets, to_over),
        (down, two, 0, HALF, to_up),
        (down, down_o, 0, FIRST, to_over),
        (up, two, HALF, kets, to_down),
        (up, up_o, 0, FIRST, to_over),
        (over, down_o, FIRST, kets, to_up),
        (over, up_o, FIRST, kets, to_down),
        (two, two_o, 0, FIRST, to_over),
        (down_o, two_o, FIRST, FIRST + QUARTER, to_up),
        (up_o, two_o, FIRST + QUARTER, kets, to_down),
    )

    def send(j, i):
        block, _, lo, hi, device = hops[i]
        hop(j, i, block, lo, hi, device).start()

    def landed(ref, sem):
        pltpu.make_async_copy(ref, ref, sem).wait()

    def arrived(j, group):
        count = sum(hi - lo for (_, _, lo, hi, _), g in zip(hops, GROUP) if g == group)
        parts_ = next(n for n in range(1, rows) if count % (n * 16) == 0 and count // n <= kets)
        landed(amps.at[j, pl.ds(0, parts_), pl.ds(0, count // parts_)], a_recv.at[j, group])

    def first(j):
        for i in (0, 1, 2):
            send(j, i)

    def second(j):
        arrived(j, 0)
        for i in (3, 7, 8, 5, 4, 6):
            send(j, i)

    def third(j):
        arrived(j, 1)
        for i in (10, 11, 9):
            send(j, i)

    def gathered(j):
        arrived(j, 2)
        arrived(j, 3)

    def site(d):
        return lax.rem(z + d, sites)

    last = chunks - 1

    def sib_sem(j, d):
        return j if j < last else last + min(d, sites - 1 - d)

    def sib_copy(j, d):
        return pltpu.make_async_remote_copy(
            src_ref=part.at[j, site(d), 1 - core], dst_ref=sib.at[j, site(d)],
            send_sem=sends.at[1], recv_sem=d_recv.at[sib_sem(j, d)],
            device_id=to_sib, device_id_type=MESH,
        )

    def multiply(j):
        for d in range(sites // 2, sites):
            both = (d, sites - 1 - d)
            left = jnp.concatenate([screened[pl.ds(site(e) * 128, 128), :] for e in both], axis=0)
            right = amps[j].reshape(rows * kets, width)
            product = jnp.dot(left, right, preferred_element_type=jnp.float32).reshape(2, 2, 64, width)
            for i, e in enumerate(both):
                part[j, site(e)] = product[i]
                sib_copy(j, e).start()

    def site_copy(j, d):
        return pltpu.make_async_remote_copy(
            src_ref=quant.at[j, d - 1], dst_ref=zin.at[j, d - 1],
            send_sem=sends.at[2], recv_sem=z_recv.at[j],
            device_id=to_site(d), device_id_type=MESH,
        )

    def scale_copy(j, d):
        return pltpu.make_async_remote_copy(
            src_ref=scale.at[j, d - 1], dst_ref=zscale.at[j, d - 1],
            send_sem=sends.at[3], recv_sem=s_recv.at[j],
            device_id=to_site(d), device_id_type=MESH,
        )

    order = [e for d in range(sites // 2, sites) for e in (d, sites - 1 - d) if e]

    def scatter(j):
        if j < last:
            with jax.named_scope("sibwait"):
                landed(sib.at[j], d_recv.at[j])
        for d in order:
            if j == last and d >= sites // 2:
                with jax.named_scope("sibwait"):
                    landed(sib.at[j, pl.ds(0, 2)], d_recv.at[sib_sem(j, d)])
            value = part[j, site(d), core] + sib[j, site(d)]
            top = jnp.maximum(jnp.max(jnp.abs(value), axis=0, keepdims=True), 1e-30)
            scale[j, d - 1] = top * (1.0 / LEVELS)
            quant[j, d - 1] = jnp.round(value * (LEVELS / top)).astype(jnp.int32).astype(jnp.int16)
            scale_copy(j, d).start()
            site_copy(j, d).start()

    def pair_copy(j):
        return pltpu.make_async_remote_copy(
            src_ref=total.at[j, pl.ds((1 - pair) * 32, 32)], dst_ref=pair_in.at[j],
            send_sem=sends.at[4], recv_sem=p_recv.at[j],
            device_id=to_pair, device_id_type=MESH,
        )

    def collect(j):
        value = part[j, z, core] + sib[j, z]
        with jax.named_scope("sitewait"):
            landed(zscale.at[j], s_recv.at[j])
            landed(zin.at[j], z_recv.at[j])
        for d in reversed(order):
            value += zin[j, d - 1].astype(jnp.int32).astype(jnp.float32) * zscale[j, d - 1]
        total[j] = value
        pair_copy(j).start()

    half = chunks * width

    def couple(j, which, ladder):
        columns = pl.ds(pl.multiple_of(which * half + j * width, width), width)
        residual = driver_v[:, columns].astype(jnp.float32) + ladder
        resid[:, columns] = residual
        scaled = (residual / (vir_col() - occ_v[columns].reshape(1, width))).astype(jnp.bfloat16)
        coupled[...] += jnp.dot(scaled, coup_v[columns, :], preferred_element_type=jnp.float32)

    def vir_col():
        n = vir_v.shape[0]
        eye = lax.broadcasted_iota(jnp.int32, (n, n), 0) == lax.broadcasted_iota(jnp.int32, (n, n), 1)
        return jnp.sum(jnp.where(eye, jnp.broadcast_to(vir_v[...].reshape(1, n), (n, n)), 0.0), axis=1, keepdims=True)

    def finish(j):
        couple(j, pair, total[j, pl.ds(pair * 32, 32)])
        with jax.named_scope("pairwait"):
            pair_copy(j).wait_recv()
        couple(j, 1 - pair, pair_in[j])

    with jax.named_scope("barrier"):
        pl.semaphore_wait(barrier, len(friends))
    landed(amps.at[:, row], load_sem.at[6])
    with jax.named_scope("first"):
        for j in range(min(AHEAD, chunks)):
            first(j)
    tell(0)

    coupled[...] = jnp.zeros_like(coupled)
    loads[0].wait()
    tiles = kept_v.shape[1]
    tile = depth // tiles
    keep = kept_v[...].astype(jnp.float32).astype(jnp.bfloat16)
    for b in range(depth // 256):
        ket = lax.broadcasted_iota(jnp.int32, (tiles, 256), 1) + b * 256
        of = lax.broadcasted_iota(jnp.int32, (tiles, 256), 0) * tile
        spread = jnp.where((ket >= of) & (ket < of + tile), 1.0, 0.0).astype(jnp.bfloat16)
        mask[:, pl.ds(b * 256, 256)] = jnp.dot(keep, spread, preferred_element_type=jnp.float32)
    loads[1].wait()

    def screen(i, carry):
        strip = pl.ds(i * tile, tile)
        keep_row = jnp.broadcast_to(mask[pl.ds(i, 1), :], (tile, depth)).astype(jnp.bfloat16)
        screened[strip, :] = screened[strip, :] * keep_row
        return carry

    with jax.named_scope("screen"):
        lax.fori_loop(0, kept_v.shape[0], screen, 0)
    def product(j):
        with jax.named_scope("gathered"):
            gathered(j)
        with jax.named_scope("dot"):
            multiply(j)

    def named(name, f):
        def call(j):
            with jax.named_scope(name):
                f(j)

        return call

    steps = {
        "S": (0, named("second", second)),
        "F": (-AHEAD, first),
        "T": (LAG_T, named("third", third)),
        "G": (LAG_G, product),
        "X": (LAG_G + 1, scatter),
        "C": (LAG_G + 3, collect),
        "E": (LAG_G + 5, finish),
    }
    done = dict.fromkeys(steps, -1)
    done["F"] = AHEAD - 1
    for s in range(chunks + LAG_G):
        for name in ORDER:
            lag, step = steps[name]
            j = s - lag
            if 0 <= j < chunks and j > done[name]:
                step(j)
                done[name] = j
        if s < sites // 2 - 1:
            told(s)
            if s + 1 < sites // 2 - 1:
                tell(s + 1)
        if s == 2:
            for c in loads[2:]:
                c.wait()
    for j in range(done["X"] + 1, chunks):
        scatter(j)
    for j in range(done["C"] + 1, chunks):
        if j == last:
            landed(amps.at[:, pl.ds(0, rows - 1)], sends.at[0])
            landed(sib, sends.at[1])
        collect(j)
        while done["E"] < j - 1:
            done["E"] += 1
            finish(done["E"])
    landed(quant, sends.at[2])
    landed(scale, sends.at[3])
    with jax.named_scope("finlast"):
        finish(last)
    with jax.named_scope("out"):
        resid[...] = resid[...] - coupled[...]
        oc = pltpu.make_async_copy(resid, out, load_sem.at[6])
        oc.start()
        oc.wait()
    with jax.named_scope("pairsent"):
        landed(pair_in, sends.at[4])


def per_device(integrals, kept_tiles, amplitudes, driver, vir_energy, occ_energy, occ_coupling):
    bra, depth = integrals.shape
    kets, half = amplitudes.shape
    rows = depth // kets
    chunks = half // WIDTH
    sites = bra // 128
    own, whole = driver.shape
    any_ = pl.BlockSpec(memory_space=pltpu.HBM)
    dma = pltpu.SemaphoreType.DMA
    numerator = pl.pallas_call(
        kernel,
        out_shape=jax.ShapeDtypeStruct((own, whole), jnp.float32),
        in_specs=[any_] * 7,
        out_specs=any_,
        scratch_shapes=[
            pltpu.VMEM((bra, depth), jnp.bfloat16),
            pltpu.VMEM(kept_tiles.shape, jnp.int32),
            pltpu.VMEM((own, whole), jnp.bfloat16),
            pltpu.VMEM((own,), jnp.float32),
            pltpu.VMEM((whole,), jnp.float32),
            pltpu.VMEM((whole, whole), jnp.bfloat16),
            pltpu.VMEM((kept_tiles.shape[0], depth), jnp.float32),
            pltpu.VMEM((chunks, rows, kets, WIDTH), jnp.bfloat16),
            pltpu.VMEM((chunks, sites, 2, 64, WIDTH), jnp.float32),
            pltpu.VMEM((chunks, sites, 64, WIDTH), jnp.float32),
            pltpu.VMEM((chunks, sites - 1, 64, WIDTH), jnp.int16),
            pltpu.VMEM((chunks, sites - 1, 1, WIDTH), jnp.float32),
            pltpu.VMEM((chunks, sites - 1, 64, WIDTH), jnp.int16),
            pltpu.VMEM((chunks, sites - 1, 1, WIDTH), jnp.float32),
            pltpu.VMEM((chunks, 64, WIDTH), jnp.float32),
            pltpu.VMEM((chunks, 32, WIDTH), jnp.float32),
            pltpu.VMEM((own, whole), jnp.float32),
            pltpu.VMEM((own, whole), jnp.float32),
            dma((7,)),
            dma((5,)),
            dma((chunks, 4)),
            dma((chunks + sites // 2,)),
            dma((chunks,)),
            dma((chunks,)),
            dma((chunks,)),
            pltpu.SemaphoreType.REGULAR((sites // 2 - 1,)),
        ],
        compiler_params=pltpu.CompilerParams(
            collective_id=0, has_side_effects=True, vmem_limit_bytes=60 * 1024 * 1024
        ),
        name="ladder",
    )(
        integrals, kept_tiles, amplitudes, driver,
        vir_energy, occ_energy, occ_coupling,
    )
    return -numerator / (vir_energy[:, None] - occ_energy[None, :])


def solution(mesh):
    place = ("row", "col", "pair")
    placed = (
        P("row", "col"),
        P("row", "col"),
        P(("col", "row"), "pair"),
        P(place, None),
        P(place),
        P(),
        P(),
    )
    return jax.shard_map(
        per_device, mesh=mesh, in_specs=placed, out_specs=P(place, None), check_vma=False
    )
```

time: 68.3 us -> 51.7 us (0.76)
  Pallas kernels: 61 us -> 49.9 us
  local copies, waits for them, and re-layouts: 6.19 us -> 0.01 us
  other arithmetic: 0.78 us -> 1.71 us
    pallas_call x1, Pallas kernels: 61 us -> 49.9 us  [per_device(): pl.pallas_call(kernel, out_shape=jax.ShapeDtypeStruct((own, whole), jnp.f...]
    unnamed x12 -> x4, local copies, waits for them, and re-layouts: 5.49 us -> 0.01 us
    div x1, other arithmetic: 0.78 us -> 1.71 us  [per_device(): return -numerator / (vir_energy[:, None] - occ_energy[None, :])]
    reshape x1 -> x0, local copies, waits for them, and re-layouts: 0.7 us -> none  [per_device(): occ_energy.reshape(1, whole)]
where the time goes in v2:
time: 51.7 us; the launch traced here: 51.6 us
  Pallas kernels  49.9 us (97%)
  other arithmetic  1.71 us (3%)
    pallas_call x1, Pallas kernels, per_device(): pl.pallas_call(kernel, out_shape=jax.ShapeDtypeStruct((own, whole), jnp.f...  49.9 us
    div x1, other arithmetic, per_device(): return -numerator / (vir_energy[:, None] - occ_energy[None, :])  1.71 us

profile of v2, /device:TPU:1, one launch (start us, length us, event | category | flops | bytes accessed | tf_op | source)
XLA Modules:
  0.0 51.6 jit_solution(8032408665546424206)
XLA Ops:
  0.0 0.0 copy-start
  0.0 0.0 copy-start.1
  0.0 49.9 %ladder.1 = f32[32,1536]{1,0:T(8,128)} custom-call(bf16[1024,2048]{1,0:T(8,128)(2,1)} %integrals.1, s32[64,128]{1,0:T(8,128)} %kept.1, bf16[256,768]{1,0:T(8,128)(2,1)} %amplitudes.1, bf16[32,1536]{1,0:T(8,128)(2,1)} %driver.1, f32[32]{0:T(128)} %vir.1, f32[1536]{0:T(1024)} %occ.1, bf16[1536,1536]{1,0:T(8,128)(2,1)} %coupling.1), custom_call_target="tpu_custom_call" | custom-call | tf_op jit(solution)/shard_map/ladder/pallas_call | solution.py:322
  49.9 0.0 copy-done
  49.9 0.0 copy-done.1
  49.9 1.7 %subtract_divide_fusion = f32[32,1536]{1,0:T(8,128)} fusion(f32[32,1536]{1,0:T(8,128)} %ladder.1, f32[1536]{0:T(1024)S(1)} %copy-done, f32[32]{0:T(128)S(1)} %copy-done.1), kind=kLoop, calls=%fused_computation | loop fusion | flops 147456 | bytes 399488 | tf_op jit(solution)/shard_map/div | solution.py:363
Async XLA Ops:
  0.0 49.9 %copy-start = (f32[1536]{0:T(1024)S(1)}, f32[1536]{0:T(1024)}, u32[]{:S(2)}) copy-start(f32[1536]{0:T(1024)} %occ.1) | copy-start | bytes 18436
  0.0 49.9 %copy-start.1 = (f32[32]{0:T(128)S(1)}, f32[32]{0:T(128)}, u32[]{:S(2)}) copy-start(f32[32]{0:T(128)} %vir.1) | copy-start | bytes 388

commit v3 on v2

--- a/solution.py
+++ b/solution.py
@@ -10,8 +10,9 @@
 FIRST = 112
 HALF = 128
 QUARTER = 64
-ORDER = "SFECXTG"
+ORDER = "SFECXTGR"
 LAG_T = 1
+FAR = 4
 LAG_G = 2
 AHEAD = 2
 LEVELS = 32000.0
@@ -21,8 +22,8 @@
 def kernel(
     integrals, kept, amplitudes, driver, vir, occ, coupling, out,
     screened, kept_v, driver_v, vir_v, occ_v, coup_v, mask, amps, part, sib, quant, scale, zin, zscale,
-    total, pair_in, resid, coupled,
-    load_sem, sends, a_recv, d_recv, z_recv, s_recv, p_recv, ready,
+    total, pair_in, far, far_scale, resid, coupled,
+    load_sem, sends, a_recv, d_recv, z_recv, s_recv, p_recv, f_recv, ready,
 ):
     chunks, rows, kets, width = amps.shape
     depth = screened.shape[1]
@@ -153,36 +154,64 @@
                 part[j, site(e)] = product[i]
                 sib_copy(j, e).start()
 
-    def site_copy(j, d):
-        return pltpu.make_async_remote_copy(
-            src_ref=quant.at[j, d - 1], dst_ref=zin.at[j, d - 1],
-            send_sem=sends.at[2], recv_sem=z_recv.at[j],
-            device_id=to_site(d), device_id_type=MESH,
-        )
-
-    def scale_copy(j, d):
-        return pltpu.make_async_remote_copy(
-            src_ref=scale.at[j, d - 1], dst_ref=zscale.at[j, d - 1],
-            send_sem=sends.at[3], recv_sem=s_recv.at[j],
-            device_id=to_site(d), device_id_type=MESH,
-        )
-
-    order = [e for d in range(sites // 2, sites) for e in (d, sites - 1 - d) if e]
+    def summed(j, d):
+        return part[j, site(d), core] + sib[j, site(d)]
+
+    def encode(j, slot, value):
+        top = jnp.maximum(jnp.max(jnp.abs(value), axis=0, keepdims=True), 1e-30)
+        scale[j, slot] = top * (1.0 / LEVELS)
+        quant[j, slot] = jnp.round(value * (LEVELS / top)).astype(jnp.int32).astype(jnp.int16)
+
+    def decode(code, factor):
+        return code.astype(jnp.int32).astype(jnp.float32) * factor
+
+    def message(j, slot, inbox, factor, lo, hi, d, group):
+        device = to_site(d)
+        return (
+            pltpu.make_async_remote_copy(
+                src_ref=scale.at[j, slot], dst_ref=zscale.at[j, factor],
+                send_sem=sends.at[3], recv_sem=s_recv.at[j, group], device_id=device, device_id_type=MESH,
+            ),
+            pltpu.make_async_remote_copy(
+                src_ref=quant.at[j, slot, pl.ds(lo, hi - lo)], dst_ref=zin.at[j, inbox, pl.ds(lo, hi - lo)],
+                send_sem=sends.at[2], recv_sem=z_recv.at[j, group], device_id=device, device_id_type=MESH,
+            ),
+        )
+
+    def post(*args):
+        for c in message(*args):
+            c.start()
+
+    def await_sib(j):
+        with jax.named_scope("sibwait"):
+            landed(sib.at[j], d_recv.at[j])
 
     def scatter(j):
-        if j < last:
-            with jax.named_scope("sibwait"):
-                landed(sib.at[j], d_recv.at[j])
-        for d in order:
-            if j == last and d >= sites // 2:
-                with jax.named_scope("sibwait"):
-                    landed(sib.at[j, pl.ds(0, 2)], d_recv.at[sib_sem(j, d)])
-            value = part[j, site(d), core] + sib[j, site(d)]
-            top = jnp.maximum(jnp.max(jnp.abs(value), axis=0, keepdims=True), 1e-30)
-            scale[j, d - 1] = top * (1.0 / LEVELS)
-            quant[j, d - 1] = jnp.round(value * (LEVELS / top)).astype(jnp.int32).astype(jnp.int16)
-            scale_copy(j, d).start()
-            site_copy(j, d).start()
+        await_sib(j)
+        encode(j, 2, summed(j, 4))
+        post(j, 2, 2, 2, 0, 32, 2, 0)
+        post(j, 2, 2, 3, 32, 64, 6, 0)
+        encode(j, 0, summed(j, 3))
+        post(j, 0, 0, 0, 0, 64, 1, 0)
+        encode(j, 1, summed(j, 5))
+        post(j, 1, 1, 1, 0, 64, 7, 0)
+        encode(j, 3, summed(j, 1))
+        post(j, 3, 3, 4, 0, 64, 1, 1)
+        encode(j, 4, summed(j, 7))
+        post(j, 4, 4, 5, 0, 64, 7, 1)
+
+    def relay(j):
+        with jax.named_scope("relaywait"):
+            landed(zscale.at[j, pl.ds(0, 4)], s_recv.at[j, 0])
+            landed(zin.at[j, pl.ds(0, 3)], z_recv.at[j, 0])
+        ahead = summed(j, 2) + decode(zin[j, 0], zscale[j, 0])
+        top = decode(zin[j, 2, 0:32], zscale[j, 2])
+        encode(j, 5, jnp.concatenate([ahead[0:32] + top, ahead[32:64]], axis=0))
+        post(j, 5, 5, 6, 0, 64, 2, 1)
+        behind = summed(j, 6) + decode(zin[j, 1], zscale[j, 1])
+        low = decode(zin[j, 2, 32:64], zscale[j, 3])
+        encode(j, 6, jnp.concatenate([behind[0:32], behind[32:64] + low], axis=0))
+        post(j, 6, 6, 7, 0, 64, 6, 1)
 
     def pair_copy(j):
         return pltpu.make_async_remote_copy(
@@ -192,14 +221,64 @@
         )
 
     def collect(j):
-        value = part[j, z, core] + sib[j, z]
+        value = summed(j, 0)
         with jax.named_scope("sitewait"):
-            landed(zscale.at[j], s_recv.at[j])
-            landed(zin.at[j], z_recv.at[j])
-        for d in reversed(order):
-            value += zin[j, d - 1].astype(jnp.int32).astype(jnp.float32) * zscale[j, d - 1]
+            landed(zscale.at[j, pl.ds(4, 4)], s_recv.at[j, 1])
+            landed(zin.at[j, pl.ds(3, 4)], z_recv.at[j, 1])
+        for i in range(4):
+            value += decode(zin[j, 3 + i], zscale[j, 4 + i])
         total[j] = value
         pair_copy(j).start()
+
+    near = chunks - FAR
+
+    def far_copies(j, d, other):
+        whom = 1 - pair if other else pair
+        device = (row, site(d) * 2 + core, whom)
+        f = j - near
+        return (
+            pltpu.make_async_remote_copy(
+                src_ref=scale.at[j, d], dst_ref=far_scale.at[f, other, d],
+                send_sem=sends.at[5 + other], recv_sem=f_recv.at[f, other], device_id=device, device_id_type=MESH,
+            ),
+            pltpu.make_async_remote_copy(
+                src_ref=quant.at[j, d, pl.ds(whom * 32, 32)], dst_ref=far.at[f, other, d],
+                send_sem=sends.at[7 + other], recv_sem=f_recv.at[f, 2 + other], device_id=device, device_id_type=MESH,
+            ),
+        )
+
+    def scatter_far(j):
+        if j < last:
+            await_sib(j)
+        for d in range(sites // 2, sites):
+            if j == last:
+                with jax.named_scope("sibwait"):
+                    landed(sib.at[j, pl.ds(0, 2)], d_recv.at[sib_sem(j, d)])
+            for e in (d, sites - 1 - d):
+                encode(j, e, summed(j, e))
+                for other in (1, 0) if e else (1,):
+                    for c in far_copies(j, e, other):
+                        c.start()
+
+    def finish_far(j):
+        f = j - near
+        for other in (0, 1):
+            first_ = 0 if other else 1
+            with jax.named_scope("farwait"):
+                landed(far_scale.at[f, other, pl.ds(first_, sites - first_)], f_recv.at[f, other])
+                landed(far.at[f, other, pl.ds(first_, sites - first_)], f_recv.at[f, 2 + other])
+            ladder = decode(far[f, other, first_], far_scale[f, other, first_])
+            for d in range(first_ + 1, sites):
+                ladder += decode(far[f, other, d], far_scale[f, other, d])
+            if not other:
+                ladder += part[j, z, core, pl.ds(pair * 32, 32)] + sib[j, z, pl.ds(pair * 32, 32)]
+            couple(j, 1 - pair if other else pair, ladder)
+
+    def far_sent():
+        for other in (0, 1):
+            first_ = 0 if other else 1
+            landed(far_scale.at[:, other, pl.ds(first_, sites - first_)], sends.at[5 + other])
+            landed(far.at[:, other, pl.ds(first_, sites - first_)], sends.at[7 + other])
 
     half = chunks * width
 
@@ -267,8 +346,9 @@
         "F": (-AHEAD, first),
         "T": (LAG_T, named("third", third)),
         "G": (LAG_G, product),
-        "X": (LAG_G + 1, scatter),
-        "C": (LAG_G + 3, collect),
+        "X": (LAG_G + 1, lambda j: scatter(j) if j < near else scatter_far(j)),
+        "R": (LAG_G + 2, relay),
+        "C": (LAG_G + 4, collect),
         "E": (LAG_G + 5, finish),
     }
     done = dict.fromkeys(steps, -1)
@@ -277,7 +357,7 @@
         for name in ORDER:
             lag, step = steps[name]
             j = s - lag
-            if 0 <= j < chunks and j > done[name]:
+            if 0 <= j < (near if name in "RCE" else chunks) and j > done[name]:
                 step(j)
                 done[name] = j
         if s < sites // 2 - 1:
@@ -285,29 +365,36 @@
             if s + 1 < sites // 2 - 1:
                 tell(s + 1)
         if s == 2:
+            pl.semaphore_signal(ready.at[sites // 2 - 1], inc=1, device_id=to_pair, device_id_type=MESH)
             for c in loads[2:]:
                 c.wait()
+    pl.semaphore_wait(ready.at[sites // 2 - 1], 1)
     for j in range(done["X"] + 1, chunks):
-        scatter(j)
-    for j in range(done["C"] + 1, chunks):
-        if j == last:
-            landed(amps.at[:, pl.ds(0, rows - 1)], sends.at[0])
-            landed(sib, sends.at[1])
-        collect(j)
-        while done["E"] < j - 1:
+        steps["X"][1](j)
+    for j in range(done["R"] + 1, near):
+        relay(j)
+    for j in range(done["C"] + 1, near):
+        while done["E"] < j - 2:
             done["E"] += 1
             finish(done["E"])
-    landed(quant, sends.at[2])
-    landed(scale, sends.at[3])
-    with jax.named_scope("finlast"):
-        finish(last)
+        collect(j)
+    landed(amps.at[:, pl.ds(0, rows - 1)], sends.at[0])
+    landed(sib, sends.at[1])
+    landed(zin, sends.at[2])
+    landed(zscale, sends.at[3])
+    for j in range(done["E"] + 1, near - 1):
+        finish(j)
+    for j in range(near, last):
+        finish_far(j)
+    finish(near - 1)
+    far_sent()
+    landed(pair_in.at[pl.ds(0, near)], sends.at[4])
+    finish_far(last)
     with jax.named_scope("out"):
         resid[...] = resid[...] - coupled[...]
         oc = pltpu.make_async_copy(resid, out, load_sem.at[6])
         oc.start()
         oc.wait()
-    with jax.named_scope("pairsent"):
-        landed(pair_in, sends.at[4])
 
 
 def per_device(integrals, kept_tiles, amplitudes, driver, vir_energy, occ_energy, occ_coupling):
@@ -335,22 +422,25 @@
             pltpu.VMEM((chunks, rows, kets, WIDTH), jnp.bfloat16),
             pltpu.VMEM((chunks, sites, 2, 64, WIDTH), jnp.float32),
             pltpu.VMEM((chunks, sites, 64, WIDTH), jnp.float32),
-            pltpu.VMEM((chunks, sites - 1, 64, WIDTH), jnp.int16),
-            pltpu.VMEM((chunks, sites - 1, 1, WIDTH), jnp.float32),
-            pltpu.VMEM((chunks, sites - 1, 64, WIDTH), jnp.int16),
-            pltpu.VMEM((chunks, sites - 1, 1, WIDTH), jnp.float32),
+            pltpu.VMEM((chunks, sites, 64, WIDTH), jnp.int16),
+            pltpu.VMEM((chunks, sites, 1, WIDTH), jnp.float32),
+            pltpu.VMEM((chunks - FAR, 7, 64, WIDTH), jnp.int16),
+            pltpu.VMEM((chunks - FAR, 8, 1, WIDTH), jnp.float32),
             pltpu.VMEM((chunks, 64, WIDTH), jnp.float32),
             pltpu.VMEM((chunks, 32, WIDTH), jnp.float32),
+            pltpu.VMEM((FAR, 2, sites, 32, WIDTH), jnp.int16),
+            pltpu.VMEM((FAR, 2, sites, 1, WIDTH), jnp.float32),
             pltpu.VMEM((own, whole), jnp.float32),
             pltpu.VMEM((own, whole), jnp.float32),
             dma((7,)),
-            dma((5,)),
+            dma((9,)),
             dma((chunks, 4)),
             dma((chunks + sites // 2,)),
+            dma((chunks, 2)),
+            dma((chunks, 2)),
             dma((chunks,)),
-            dma((chunks,)),
-            dma((chunks,)),
-            pltpu.SemaphoreType.REGULAR((sites // 2 - 1,)),
+            dma((FAR, 4)),
+            pltpu.SemaphoreType.REGULAR((sites // 2,)),
         ],
         compiler_params=pltpu.CompilerParams(
             collective_id=0, has_side_effects=True, vmem_limit_bytes=60 * 1024 * 1024

time: 51.7 us -> 50.9 us (0.985)
  Pallas kernels: 49.9 us -> 49.1 us
    pallas_call x1, Pallas kernels: 49.9 us -> 49.1 us  [per_device(): pl.pallas_call(kernel, out_shape=jax.ShapeDtypeStruct((own, whole), jnp.f...]
where the time goes in v3:
time: 50.9 us
  Pallas kernels  49.1 us (96%)
  other arithmetic  1.71 us (3%)
    pallas_call x1, Pallas kernels, per_device(): pl.pallas_call(kernel, out_shape=jax.ShapeDtypeStruct((own, whole), jnp.f...  49.1 us
    div x1, other arithmetic, per_device(): return -numerator / (vir_energy[:, None] - occ_energy[None, :])  1.71 us

profile of v3, /device:TPU:1, one launch (start us, length us, event | category | flops | bytes accessed | tf_op | source)
XLA Modules:
  0.0 50.9 jit_solution(17720477577799381557)
XLA Ops:
  0.0 0.0 copy-start
  0.0 0.0 copy-start.1
  0.0 49.1 %ladder.1 = f32[32,1536]{1,0:T(8,128)} custom-call(bf16[1024,2048]{1,0:T(8,128)(2,1)} %integrals.1, s32[64,128]{1,0:T(8,128)} %kept.1, bf16[256,768]{1,0:T(8,128)(2,1)} %amplitudes.1, bf16[32,1536]{1,0:T(8,128)(2,1)} %driver.1, f32[32]{0:T(128)} %vir.1, f32[1536]{0:T(1024)} %occ.1, bf16[1536,1536]{1,0:T(8,128)(2,1)} %coupling.1), custom_call_target="tpu_custom_call" | custom-call | tf_op jit(solution)/shard_map/ladder/pallas_call | solution.py:409
  49.1 0.0 copy-done
  49.1 0.0 copy-done.1
  49.1 1.7 %subtract_divide_fusion = f32[32,1536]{1,0:T(8,128)} fusion(f32[32,1536]{1,0:T(8,128)} %ladder.1, f32[1536]{0:T(1024)S(1)} %copy-done, f32[32]{0:T(128)S(1)} %copy-done.1), kind=kLoop, calls=%fused_computation | loop fusion | flops 147456 | bytes 399488 | tf_op jit(solution)/shard_map/div | solution.py:453
Async XLA Ops:
  0.0 49.1 %copy-start = (f32[1536]{0:T(1024)S(1)}, f32[1536]{0:T(1024)}, u32[]{:S(2)}) copy-start(f32[1536]{0:T(1024)} %occ.1) | copy-start | bytes 18436
  0.0 49.1 %copy-start.1 = (f32[32]{0:T(128)S(1)}, f32[32]{0:T(128)}, u32[]{:S(2)}) copy-start(f32[32]{0:T(128)} %vir.1) | copy-start | bytes 388

commit v4 on v3

--- a/solution.py
+++ b/solution.py
@@ -10,7 +10,7 @@
 FIRST = 112
 HALF = 128
 QUARTER = 64
-ORDER = "SFECXTGR"
+ORDER = "SFXTGRCE"
 LAG_T = 1
 FAR = 4
 LAG_G = 2
@@ -349,7 +349,7 @@
         "X": (LAG_G + 1, lambda j: scatter(j) if j < near else scatter_far(j)),
         "R": (LAG_G + 2, relay),
         "C": (LAG_G + 4, collect),
-        "E": (LAG_G + 5, finish),
+        "E": (LAG_G + 20, finish),
     }
     done = dict.fromkeys(steps, -1)
     done["F"] = AHEAD - 1

time: 50.9 us -> 51.4 us (level)
  no operation moved by 1% of the time
where the time goes in v4:
time: 51.4 us; the launch traced here: 51.3 us
  Pallas kernels  49.6 us (96%)
  other arithmetic  1.71 us (3%)
    pallas_call x1, Pallas kernels, per_device(): pl.pallas_call(kernel, out_shape=jax.ShapeDtypeStruct((own, whole), jnp.f...  49.6 us
    div x1, other arithmetic, per_device(): return -numerator / (vir_energy[:, None] - occ_energy[None, :])  1.71 us

profile of v4, /device:TPU:1, one launch (start us, length us, event | category | flops | bytes accessed | tf_op | source)
XLA Modules:
  0.0 51.3 jit_solution(2248891851906286150)
XLA Ops:
  0.0 0.0 copy-start
  0.0 0.0 copy-start.1
  0.0 49.6 %ladder.1 = f32[32,1536]{1,0:T(8,128)} custom-call(bf16[1024,2048]{1,0:T(8,128)(2,1)} %integrals.1, s32[64,128]{1,0:T(8,128)} %kept.1, bf16[256,768]{1,0:T(8,128)(2,1)} %amplitudes.1, bf16[32,1536]{1,0:T(8,128)(2,1)} %driver.1, f32[32]{0:T(128)} %vir.1, f32[1536]{0:T(1024)} %occ.1, bf16[1536,1536]{1,0:T(8,128)(2,1)} %coupling.1), custom_call_target="tpu_custom_call" | custom-call | tf_op jit(solution)/shard_map/ladder/pallas_call | solution.py:409
  49.6 0.0 copy-done
  49.6 0.0 copy-done.1
  49.6 1.7 %subtract_divide_fusion = f32[32,1536]{1,0:T(8,128)} fusion(f32[32,1536]{1,0:T(8,128)} %ladder.1, f32[1536]{0:T(1024)S(1)} %copy-done, f32[32]{0:T(128)S(1)} %copy-done.1), kind=kLoop, calls=%fused_computation | loop fusion | flops 147456 | bytes 399488 | tf_op jit(solution)/shard_map/div | solution.py:453
Async XLA Ops:
  0.0 49.6 %copy-start = (f32[1536]{0:T(1024)S(1)}, f32[1536]{0:T(1024)}, u32[]{:S(2)}) copy-start(f32[1536]{0:T(1024)} %occ.1) | copy-start | bytes 18436
  0.0 49.6 %copy-start.1 = (f32[32]{0:T(128)S(1)}, f32[32]{0:T(128)}, u32[]{:S(2)}) copy-start(f32[32]{0:T(128)} %vir.1) | copy-start | bytes 388
